TPU v7x, 32 devices: a whole 2x2x4 slice. The times are simulated.
32 devices in a mesh: section: 4 (over y, x), expert: 8 (over z, core).
Axes of the slice: x: 2, y: 2, z: 4, core: 2. Of those that a mesh axis runs over, the one named last changes fastest.
Arguments:
- section_inputs: float32 [4, 1024, 2048], P('section', 'expert'), may hold values from -6 to 6
- stored_inputs: float32 [4, 1024, 2048], P('section', 'expert'), may hold values from -6 to 6
- out_grads: bfloat16 [4, 1024, 2048], P('section', 'expert'), may hold values from -6 to 6
- fwd_routes: int32 [4, 1024, 2], P('section', 'expert'), may hold values from 0 to 3, all different within a row; in each aligned block of 128 rows (0 to 127, 128 to 255, ..., all dimensions but the last counted through in order) at most 80 rows name the same one
- fwd_gates: float32 [4, 1024, 2], P('section', 'expert'), may hold values from 0.2 to 1
- fwd_modulation: float32 [4, 3, 2048], P('section'), may hold values from -3 to 3
- bwd_routes: int32 [4, 1024, 2], P('section', 'expert'), may hold values from 0 to 3, all different within a row; in each aligned block of 128 rows (0 to 127, 128 to 255, ..., all dimensions but the last counted through in order) at most 80 rows name the same one
- bwd_gates: float32 [4, 1024, 2], P('section', 'expert'), may hold values from 0.2 to 1
- bwd_modulation: float32 [4, 3, 2048], P('section'), may hold values from -3 to 3
- up_weight: bfloat16 [4, 8, 2048, 1024], P('section', 'expert'), may hold values from -0.125 to 0.125
- down_weight: bfloat16 [4, 8, 1024, 2048], P('section', 'expert'), may hold values from -0.125 to 0.125
Outputs:
- next_inputs: float32 [4, 1024, 2048], P('section', 'expert')
- input_grads: bfloat16 [4, 1024, 2048], P('section', 'expert')
Inputs may be any that keep to these rules, and one draw needn't show every extreme that they name: `fwd_routes`: A token names two different experts. In the rows of one index of expert (aligned blocks of 128 rows of a section) no expert is named more than 80 times, a bound that some block reaches. `bwd_routes`: A token names two different experts. In the rows of one index of expert (aligned blocks of 128 rows of a section) no expert is named more than 80 times, a bound that some block reaches.
All inputs are finite; a program needn't handle non-finite values.
Results may differ from a plain program's by a relative error of at most 0.0042.
Values may be sent and summed in bfloat16 or wider, within the bound.
A program may use at most 128 MiB of HBM per device.

v0:
```python
import functools

import jax
import jax.numpy as jnp
from jax import lax
from jax.experimental import pallas as pl
from jax.experimental.pallas import tpu as pltpu
from jax.sharding import PartitionSpec as P

norm_eps = 1e-06
F32, BF16 = jnp.float32, jnp.bfloat16
MESH = pl.DeviceIdType.MESH
ROOT, CUBE = 0.7978845608028654, 0.044715


def flip(index, mask, bits):
    total = 0
    for b in range(bits):
        bit = (index // (1 << b)) % 2
        total = total + (1 << b) * (1 - bit if mask >> b & 1 else bit)
    return total


def dot(a, b, ca=1, cb=0):
    return lax.dot_general(a, b, (((ca,), (cb,)), ((), ())), preferred_element_type=F32)


def slot_masks(routes, capacity, slots):
    count = routes.shape[0]
    lanes = lax.broadcasted_iota(jnp.int32, (count, 128), 1)
    hits = [routes[:, k : k + 1] == lanes for k in range(2)]
    choose = jnp.where(hits[0] | hits[1], 1.0, 0.0).astype(BF16)
    row = lax.broadcasted_iota(jnp.int32, (count, count), 0)
    col = lax.broadcasted_iota(jnp.int32, (count, count), 1)
    before = dot(jnp.where(col < row, 1.0, 0.0).astype(BF16), choose)
    places = lax.broadcasted_iota(jnp.int32, (count, slots), 1)
    masks = []
    for k in range(2):
        rank = jnp.sum(jnp.where(hits[k], before, 0.0), axis=1, keepdims=True)
        masks.append(places == routes[:, k : k + 1] * capacity + rank.astype(jnp.int32))
    return masks


def kernel(
    sections, units, capacity,
    x_ref, st_ref, og_ref, fr_ref, fg_ref, fm_ref, br_ref, bg_ref, bm_ref, up_hbm, down_hbm,
    next_ref, grad_ref,
    up, down, snd_f, snd_r, snd_g, rcv_f, rcv_r, rcv_g, act, dgelu,
    px_f, px_b, pin_f, pin_b, ret_f, ret_b, rr_f, rr_b,
    hid, pair0, pair1, normed_b, inv_b, out_f, dh, out_b,
    w_sem, in_send, in_recv, fw_send, fw_recv, px_send, px_recv, rt_send, rt_recv,
    sf_send, sf_recv, sb_send, sb_recv,
):
    s, me = lax.axis_index("section"), lax.axis_index("expert")
    experts = units // 2
    bits = units.bit_length() - 1
    chip, core = me // 2, me % 2
    count, width = x_ref.shape
    half = width // 2
    hidden_units = up.shape[1]
    rows = units * capacity
    slots = experts * capacity
    tile = 256
    group = 16
    order = list(range(1, units))
    peer = {k: flip(me, k, bits) for k in order}

    w_up = pltpu.make_async_copy(up_hbm, up, w_sem.at[0])
    w_down = pltpu.make_async_copy(down_hbm, down, w_sem.at[1])
    w_up.start()
    w_down.start()

    barrier = pltpu.get_barrier_semaphore()
    for k in order:
        pl.semaphore_signal(barrier, inc=1, device_id=(s, peer[k]), device_id_type=MESH)
    for step in (1, sections - 1):
        pl.semaphore_signal(
            barrier, inc=1, device_id=((s + step) % sections, me), device_id_type=MESH
        )

    def remote(src, dst, send, recv, section, unit):
        return pltpu.make_async_remote_copy(
            src_ref=src, dst_ref=dst, send_sem=send, recv_sem=recv,
            device_id=(section, unit), device_id_type=MESH,
        )

    def inbound(phase, snd, rcv):
        copies = {}
        for k in order:
            d = peer[k]
            if k == 1:
                src, dst = snd.at[chip], rcv.at[:, me]
            else:
                src, dst = snd.at[d // 2, d % 2], rcv.at[d % 2, me]
            copies[k] = remote(src, dst, in_send.at[phase, k], in_recv.at[phase, k], s, d)
        return copies

    def hand_on(phase, rcv):
        copies = {}
        for k in order:
            if k > 1:
                block = rcv.at[core, peer[k]]
                copies[k] = remote(
                    block, block, fw_send.at[phase, k], fw_recv.at[phase, k], s, peer[1]
                )
        return copies

    def keep_own(snd, rcv):
        for h in range(2):
            rcv[h, me] = snd[chip, h]

    def receive(ins, fws):
        for k in order:
            ins[k].wait_recv()
            if k > 1:
                fws[k].start()
        for k in order:
            if k > 1:
                fws[k].wait_recv()

    def normalise(src, mod, keep):
        @pl.loop(0, count // group)
        def _(i):
            at = pl.ds(pl.multiple_of(i * group, group), group)
            x = src[at, :]
            centered = x - jnp.mean(x, axis=1, keepdims=True)
            inv = lax.rsqrt(jnp.mean(centered * centered, axis=1, keepdims=True) + norm_eps)
            normed = centered * inv
            hid[at, :] = (normed * (1.0 + mod[1:2, :]) + mod[0:1, :]).astype(BF16)
            if keep:
                normed_b[at, :] = normed
                inv_b[at, :] = jnp.broadcast_to(inv, (group, 128))

    def pack(terms, snd):
        for h in range(2):
            @pl.loop(0, half // tile)
            def _(n):
                src = pl.ds(pl.multiple_of(h * half + n * tile, tile), tile)
                value = sum(dot(mask, ref[:, src], 0, 0) for mask, ref in terms).astype(BF16)
                for e in range(experts):
                    snd[e, h, :, pl.ds(pl.multiple_of(n * tile, tile), tile)] = value[
                        e * capacity : (e + 1) * capacity, :
                    ]

    def onehot(mask):
        return jnp.where(mask, 1.0, 0.0).astype(BF16)

    normalise(x_ref, fm_ref, False)
    fwd = slot_masks(fr_ref[...], capacity, slots)
    pack([(onehot(fwd[0] | fwd[1]), hid)], snd_f)
    pl.semaphore_wait(barrier, units + 1)
    in_f, fw_f = inbound(0, snd_f, rcv_f), hand_on(0, rcv_f)
    for k in order:
        in_f[k].start()
    keep_own(snd_f, rcv_f)

    normalise(st_ref, bm_ref, True)
    bwd = slot_masks(br_ref[...], capacity, slots)
    bwd_hot = [onehot(mask) for mask in bwd]
    pack([(bwd_hot[0] + bwd_hot[1], hid)], snd_r)
    in_r, fw_r = inbound(1, snd_r, rcv_r), hand_on(1, rcv_r)
    for k in order:
        in_r[k].start()
    keep_own(snd_r, rcv_r)

    @pl.loop(0, count // group)
    def _(i):
        at = pl.ds(pl.multiple_of(i * group, group), group)
        scaled = bm_ref[2:3, :] * og_ref[at, :].astype(F32)
        pair0[at, :] = (bg_ref[at, 0:1] * scaled).astype(BF16)
        pair1[at, :] = (bg_ref[at, 1:2] * scaled).astype(BF16)

    pack([(bwd_hot[0], pair0), (bwd_hot[1], pair1)], snd_g)
    in_g, fw_g = inbound(2, snd_g, rcv_g), hand_on(2, rcv_g)
    for k in order:
        in_g[k].start()
    keep_own(snd_g, rcv_g)

    def flat(ref, h):
        return ref[h].reshape(rows, half)

    def cols(n, base=0):
        return pl.ds(pl.multiple_of(base + n * tile, tile), tile)

    def exchange(phase, px, pin, ret, result):
        def fill(dst, h):
            @pl.loop(0, half // tile)
            def _(n):
                value = result(h, n).astype(BF16).reshape(units, capacity, tile)
                dst[:, :, cols(n)] = value

        fill(px, 1 - core)
        swap = remote(px, pin, px_send.at[phase], px_recv.at[phase], s, peer[1])
        swap.start()
        fill(ret, core)
        swap.wait_recv()

        @pl.loop(0, units)
        def _(u):
            ret[u] = (ret[u].astype(F32) + pin[u].astype(F32)).astype(BF16)

        return swap

    def give_back(phase, ret, rr):
        copies = {}
        for k in order:
            copies[k] = remote(
                ret.at[peer[k]], rr.at[core, chip],
                rt_send.at[phase, k], rt_recv.at[phase, k], s, peer[k],
            )
            copies[k].start()
        rr[core, chip] = ret[me]
        return copies

    receive(in_f, fw_f)
    w_up.wait()
    w_down.wait()

    @pl.loop(0, hidden_units // tile)
    def _(n):
        pre = dot(flat(rcv_f, 0), up[:half, cols(n)]) + dot(flat(rcv_f, 1), up[half:, cols(n)])
        t = jnp.tanh(ROOT * (pre + CUBE * pre * pre * pre))
        act[:, cols(n)] = (0.5 * pre * (1.0 + t)).astype(BF16)

    swap_f = exchange(
        0, px_f, pin_f, ret_f, lambda h, n: dot(act[...], down[:, cols(n, h * half)])
    )
    back_f = give_back(0, ret_f, rr_f)

    receive(in_r, fw_r)

    @pl.loop(0, hidden_units // tile)
    def _(n):
        pre = dot(flat(rcv_r, 0), up[:half, cols(n)]) + dot(flat(rcv_r, 1), up[half:, cols(n)])
        t = jnp.tanh(ROOT * (pre + CUBE * pre * pre * pre))
        slope = ROOT * (1.0 + 3.0 * CUBE * pre * pre)
        dgelu[:, cols(n)] = 0.5 * (1.0 + t) + 0.5 * pre * (1.0 - t * t) * slope

    receive(in_g, fw_g)

    @pl.loop(0, hidden_units // tile)
    def _(n):
        back = dot(flat(rcv_g, 0), down[cols(n), :half], 1, 1) + dot(
            flat(rcv_g, 1), down[cols(n), half:], 1, 1
        )
        act[:, cols(n)] = (back * dgelu[:, cols(n)]).astype(BF16)

    swap_b = exchange(
        1, px_b, pin_b, ret_b, lambda h, n: dot(act[...], up[cols(n, h * half), :], 1, 1)
    )
    back_b = give_back(1, ret_b, rr_b)

    weight = sum(jnp.where(fwd[k], fg_ref[:, k : k + 1], 0.0) for k in range(2))
    high = weight.astype(BF16)
    low = (weight - high.astype(F32)).astype(BF16)
    for k in order:
        back_f[k].wait_recv()
    sends_f = []
    for h in range(2):
        side = pl.ds(h * half, half)

        @pl.loop(0, half // tile)
        def _(n):
            got = rr_f[h, :, :, cols(n)].reshape(slots, tile)
            moe = dot(high, got) + dot(low, got)
            at = cols(n, h * half)
            out_f[:, at] = x_ref[:, at] + fm_ref[2:3, at] * moe

        copy = remote(
            out_f.at[:, side], next_ref.at[:, side], sf_send.at[h], sf_recv.at[h],
            (s + 1) % sections, me,
        )
        sends_f.append(copy)

        @pl.when(s < sections - 1)
        def _():
            copy.start()

    @pl.when(s == 0)
    def _():
        next_ref[...] = jnp.zeros_like(next_ref)

    @pl.when(s == sections - 1)
    def _():
        grad_ref[...] = jnp.zeros_like(grad_ref)

    for k in order:
        back_b[k].wait_recv()
    both = bwd_hot[0] + bwd_hot[1]
    for h in range(2):
        @pl.loop(0, half // tile)
        def _(n):
            got = rr_b[h, :, :, cols(n)].reshape(slots, tile)
            dh[:, cols(n, h * half)] = dot(both, got)

    pieces = 4
    part = count // pieces
    sends_b = []
    for p in range(pieces):
        @pl.loop(0, part // group)
        def _(i):
            at = pl.ds(pl.multiple_of(p * part + i * group, group), group)
            dnorm = dh[at, :] * (1.0 + bm_ref[1:2, :])
            normed = normed_b[at, :]
            one = jnp.mean(dnorm, axis=1, keepdims=True)
            two = jnp.mean(dnorm * normed, axis=1, keepdims=True)
            out_b[at, :] = (
                og_ref[at, :].astype(F32) + (dnorm - one - normed * two) * inv_b[at, 0:1]
            ).astype(BF16)

        piece = pl.ds(p * part, part)
        copy = remote(
            out_b.at[piece], grad_ref.at[piece], sb_send.at[p], sb_recv.at[p],
            (s + sections - 1) % sections, me,
        )
        sends_b.append(copy)

        @pl.when(s > 0)
        def _():
            copy.start()

    for copies in (in_f, in_r, in_g, fw_f, fw_r, fw_g, back_f, back_b):
        for copy in copies.values():
            copy.wait_send()
    swap_f.wait_send()
    swap_b.wait_send()

    @pl.when(s < sections - 1)
    def _():
        for copy in sends_f:
            copy.wait_send()
        for copy in sends_b:
            copy.wait_recv()

    @pl.when(s > 0)
    def _():
        for copy in sends_f:
            copy.wait_recv()
        for copy in sends_b:
            copy.wait_send()


def on_device(
    section_inputs,
    stored_inputs,
    out_grads,
    fwd_routes,
    fwd_gates,
    fwd_modulation,
    bwd_routes,
    bwd_gates,
    bwd_modulation,
    up_weight,
    down_weight,
):
    sections, units = lax.axis_size("section"), lax.axis_size("expert")
    experts = units // 2
    count, width = section_inputs.shape[1:]
    hidden_units = up_weight.shape[3]
    half = width // 2
    capacity = -(-min(count, 5 * count // (2 * experts)) // 16) * 16
    rows = units * capacity

    def vmem(dtype, *shape):
        return pltpu.VMEM(shape, dtype)

    def dma(*shape):
        return pltpu.SemaphoreType.DMA(shape)

    scratch = [
        vmem(BF16, width, hidden_units),
        vmem(BF16, hidden_units, width),
        *[vmem(BF16, experts, 2, capacity, half)] * 3,
        *[vmem(BF16, 2, units, capacity, half)] * 3,
        vmem(BF16, rows, hidden_units),
        vmem(F32, rows, hidden_units),
        *[vmem(BF16, units, capacity, half)] * 6,
        *[vmem(BF16, 2, experts, capacity, half)] * 2,
        *[vmem(BF16, count, width)] * 3,
        vmem(F32, count, width),
        vmem(F32, count, 128),
        *[vmem(F32, count, width)] * 2,
        vmem(BF16, count, width),
        dma(2),
        *[dma(3, units)] * 4,
        *[dma(2)] * 2,
        *[dma(2, units)] * 2,
        *[dma(2)] * 2,
        *[dma(4)] * 2,
    ]
    in_vmem = pl.BlockSpec(memory_space=pltpu.VMEM)
    in_hbm = pl.BlockSpec(memory_space=pl.ANY)
    flops = 10 * rows * width * hidden_units
    next_inputs, input_grads = pl.pallas_call(
        functools.partial(kernel, sections, units, capacity),
        out_shape=(
            jax.ShapeDtypeStruct((count, width), F32),
            jax.ShapeDtypeStruct((count, width), BF16),
        ),
        in_specs=[in_vmem] * 9 + [in_hbm] * 2,
        out_specs=(in_vmem, in_vmem),
        scratch_shapes=scratch,
        compiler_params=pltpu.CompilerParams(
            collective_id=0, has_side_effects=True, vmem_limit_bytes=67043328
        ),
        cost_estimate=pl.CostEstimate(
            flops=flops, bytes_accessed=4 * width * hidden_units, transcendentals=0
        ),
    )(
        section_inputs[0], stored_inputs[0], out_grads[0], fwd_routes[0], fwd_gates[0],
        fwd_modulation[0], bwd_routes[0], bwd_gates[0], bwd_modulation[0],
        up_weight[0, 0], down_weight[0, 0],
    )
    return next_inputs[None], input_grads[None]


def solution(mesh):
    tokens = P("section", "expert", None)
    shared = P("section", None, None)
    weights = P("section", "expert", None, None)
    placed = (tokens,) * 5 + (shared,) + (tokens,) * 2 + (shared,) + (weights,) * 2
    return jax.shard_map(
        on_device,
        mesh=mesh,
        in_specs=placed,
        out_specs=(tokens, tokens),
        check_vma=False,
    )
```

profile of v0, /device:TPU:14, one launch (start us, length us, event | category | flops | bytes accessed | tf_op | source)
XLA Modules:
  0.0 176.0 jit_solution(10593744077870555965)
XLA Ops:
  0.6 1.4 copy.13
  2.0 1.4 copy.14
  3.5 1.4 copy.15
  4.9 1.4 copy.16
  6.3 1.4 copy_bitcast_fusion
  7.6 164.2 %shard_map.122 = (f32[128,2048]{1,0:T(8,128)}, bf16[128,2048]{1,0:T(8,128)(2,1)}) custom-call(f32[128,2048]{1,0:T(8,128)} %bitcast.23, f32[128,2048]{1,0:T(8,128)} %bitcast.24, bf16[128,2048]{1,0:T(8,128)(2,1)} %bitcast.25, s32[128,2]{1,0:T(8,128)} %bitcast.17, f32[128,2]{1,0:T(8,128)} %bitcast.18, f32[3,2048]{1,0:T(4,128)} %get-tuple-element.7.fm_ref, ...), custom_call_target="tpu_custom_call" | custom-call | flops 13421772800 | bytes 8388608 | tf_op jit(solution)/shard_map/pallas_call | solution.py:394
  171.9 2.3 %copy.23 = f32[1,128,2048]{2,1,0:T(8,128)} copy(f32[1,128,2048]{2,1,0:T(8,128)} %bitcast.15) | data formatting | bytes 2097152
  174.2 1.9 %copy.24 = bf16[1,128,2048]{2,1,0:T(8,128)(2,1)} copy(bf16[1,128,2048]{2,1,0:T(8,128)(2,1)} %bitcast.16) | data formatting | bytes 1048576
where the time goes:
time: 179 us; the launch traced here: 176 us
  Pallas kernels  164 us (92%)
  local copies, waits for them, and re-layouts  11.2 us (6%)
    pallas_call x1, Pallas kernels, on_device(): pl.pallas_call(functools.partial(kernel, sections, units, capacity), out_...  164 us
    unnamed x7, local copies, waits for them, and re-layouts  11.2 us

commit v1 on v0

--- a/solution.py
+++ b/solution.py
@@ -41,7 +41,7 @@
     return masks
 
 
-def kernel(
+def many_chips(
     sections, units, capacity,
     x_ref, st_ref, og_ref, fr_ref, fg_ref, fm_ref, br_ref, bg_ref, bm_ref, up_hbm, down_hbm,
     next_ref, grad_ref,
@@ -340,7 +340,7 @@
             copy.wait_send()
 
 
-def on_device(
+def run_many(
     section_inputs,
     stored_inputs,
     out_grads,
@@ -392,7 +392,7 @@
     in_hbm = pl.BlockSpec(memory_space=pl.ANY)
     flops = 10 * rows * width * hidden_units
     next_inputs, input_grads = pl.pallas_call(
-        functools.partial(kernel, sections, units, capacity),
+        functools.partial(many_chips, sections, units, capacity),
         out_shape=(
             jax.ShapeDtypeStruct((count, width), F32),
             jax.ShapeDtypeStruct((count, width), BF16),
@@ -414,6 +414,666 @@
     return next_inputs[None], input_grads[None]
 
 
+def two_sided(
+    sections, units, capacity, chunks, pieces,
+    x_hbm, st_hbm, og_hbm, fr_ref, fg_ref, fm_ref, br_ref, bg_ref, bm_ref, up_hbm, down_hbm,
+    next_ref, grad_ref,
+    up, down, x_v, x_prev, st_v, dense, near, cross, snd_p, relay, rows, act, agrad,
+    res, ret_p, ret_x, comb, den, normed_b, inv_b, m_out, m_in, dh, out_b,
+    meta, picks, gate,
+    load_sem, w_send, w_recv, meta_send, meta_recv, x_send, x_recv, near_send, near_recv,
+    cross_send, cross_recv, part_send, part_recv, relay_send, relay_recv,
+    retp_send, retp_recv, retx_send, retx_recv, den_send, den_recv,
+    sf_send, sf_recv, sb_send, sb_recv,
+):
+    s, me = lax.axis_index("section"), lax.axis_index("expert")
+    z, c = me // 2, me % 2
+    odd, side = z % 2, z // 2
+    inner = odd + side - 2 * odd * side
+    seat = 1 - inner
+    partner = z + 1 - 2 * odd
+    crossing = [2 - side, 3 - 3 * side]
+    is_inner, is_outer = inner == 1, inner == 0
+    count, width = x_v.shape
+    hidden = up.shape[2]
+    every = 4 * capacity
+    tile, group = 256, 16
+    chunk, piece = width // chunks, width // pieces
+    OG, HB, HF = 0, 1, 2
+    FWD, BWD = 0, 1
+    scope = jax.named_scope
+
+    def unit(chip):
+        return 2 * chip + c
+
+    def remote(src, dst, send, recv, section, to):
+        return pltpu.make_async_remote_copy(
+            src_ref=src, dst_ref=dst, send_sem=send, recv_sem=recv,
+            device_id=(section, to), device_id_type=MESH,
+        )
+
+    def cols(n, size):
+        return pl.ds(pl.multiple_of(n * size, size), size)
+
+    loads = [
+        pltpu.make_async_copy(og_hbm, dense.at[OG], load_sem.at[0]),
+        pltpu.make_async_copy(st_hbm, st_v, load_sem.at[1]),
+        pltpu.make_async_copy(x_hbm, x_v, load_sem.at[2]),
+        pltpu.make_async_copy(up_hbm, up.at[c], load_sem.at[3]),
+        pltpu.make_async_copy(down_hbm, down.at[c], load_sem.at[4]),
+    ]
+    for load in loads[:3]:
+        load.start()
+
+    barrier = pltpu.get_barrier_semaphore()
+    for chip in (partner, crossing[0], crossing[1]):
+        pl.semaphore_signal(barrier, inc=1, device_id=(s, unit(chip)), device_id_type=MESH)
+    twin = me + 1 - 2 * c
+    pl.semaphore_signal(barrier, inc=1, device_id=(s, twin), device_id_type=MESH)
+    for step in (1, sections - 1):
+        pl.semaphore_signal(
+            barrier, inc=1, device_id=((s + step) % sections, me), device_id_type=MESH
+        )
+
+    meta[0, 0:2, :] = fr_ref[...].astype(F32)
+    meta[0, 2:4, :] = fg_ref[...]
+    meta[0, 4:6, :] = br_ref[...].astype(F32)
+    meta[0, 6:8, :] = bg_ref[...]
+
+    metas = [
+        remote(meta.at[0], meta.at[1], meta_send.at[0], meta_recv.at[0], s, unit(partner)),
+        remote(
+            meta.at[0], meta.at[2 + seat], meta_send.at[1], meta_recv.at[1 + seat],
+            s, unit(crossing[0]),
+        ),
+        remote(
+            meta.at[0], meta.at[2 + seat], meta_send.at[2], meta_recv.at[1 + seat],
+            s, unit(crossing[1]),
+        ),
+    ]
+    shares = w_send.shape[1]
+
+    def twin_copy(w, p, slot):
+        src, dst = ((up_hbm, up), (down_hbm, down))[w]
+        size = src.shape[0] // shares
+        at = pl.ds(p * size, size)
+        return remote(src.at[at], dst.at[slot, at], w_send.at[w, p], w_recv.at[w, p], s, twin)
+
+    def near_copy(q, n):
+        at = cols(n, chunk)
+        return remote(
+            dense.at[q, :, at], near.at[q, :, at],
+            near_send.at[q, n], near_recv.at[q, n], s, unit(partner),
+        )
+
+    def cross_copy(q, i, n):
+        at = cols(n, chunk)
+        src = dense if i == 0 else near
+        return remote(
+            src.at[q, :, at], cross.at[q, i, :, at],
+            cross_send.at[q, i, n], cross_recv.at[q, i, n], s, unit(crossing[0]),
+        )
+
+    def part_copy(q, n):
+        at = cols(n, chunk)
+        return remote(
+            snd_p.at[q, :, at], rows.at[q, 1, :, at],
+            part_send.at[q, n], part_recv.at[q, n], s, unit(partner),
+        )
+
+    def relay_copy(q, i, n):
+        at = cols(n, chunk)
+        return remote(
+            relay.at[q, i, :, at], rows.at[q, 2 + i, :, at],
+            relay_send.at[q, i, n], relay_recv.at[q, i, n], s, unit(partner),
+        )
+
+    def retp_copy(r, n):
+        at = cols(n, piece)
+        return remote(
+            res.at[r, 1, :, at], ret_p.at[r, :, at],
+            retp_send.at[r, n], retp_recv.at[r, n], s, unit(partner),
+        )
+
+    def retx_copy(r, i, n):
+        at = cols(n, piece)
+        return remote(
+            res.at[r, 2 + i, :, at], ret_x.at[r, i, :, at],
+            retx_send.at[r, i, n], retx_recv.at[r, i, n], s, unit(partner),
+        )
+
+    def den_copy(r, i, n):
+        at = cols(n, piece)
+        return remote(
+            comb.at[r, i, :, at], den.at[r, :, at],
+            den_send.at[r, i, n], den_recv.at[r, n], s, unit(crossing[i]),
+        )
+
+    x_copy = remote(x_v, x_prev, x_send, x_recv, (s + 1) % sections, me)
+
+    def ahead_copy(n):
+        at = cols(n, piece)
+        return remote(
+            m_out.at[:, at], m_in.at[:, at], sf_send.at[n], sf_recv.at[n],
+            (s + 1) % sections, me,
+        )
+
+    parts = sb_send.shape[0]
+    part = count // parts
+
+    def back_copy(p):
+        at = cols(p, part)
+        return remote(
+            out_b.at[at], grad_ref.at[at], sb_send.at[p], sb_recv.at[p],
+            (s + sections - 1) % sections, me,
+        )
+
+    def each_chunk(body):
+        pl.loop(0, chunks)(body)
+
+    def each_piece(body):
+        pl.loop(0, pieces)(body)
+
+    row16 = lax.broadcasted_iota(jnp.int32, (16, count), 0)
+    named = jnp.where(row16 % 2 == 0, z, partner).astype(F32)
+    forward = row16 < 2
+    earlier = lax.broadcasted_iota(jnp.int32, (count, count), 0)
+    later = lax.broadcasted_iota(jnp.int32, (count, count), 1)
+    upper = jnp.where(earlier < later, 1.0, 0.0).astype(BF16)
+    places = lax.broadcasted_iota(jnp.int32, (capacity, count), 0).astype(F32)
+
+    def find(j):
+        first = jnp.where(forward, meta[j, 0:1, :], meta[j, 4:5, :]) == named
+        second = jnp.where(forward, meta[j, 1:2, :], meta[j, 5:6, :]) == named
+        weight = jnp.where(
+            first,
+            jnp.where(forward, meta[j, 2:3, :], meta[j, 6:7, :]),
+            jnp.where(forward, meta[j, 3:4, :], meta[j, 7:8, :]),
+        )
+        chosen = first | second
+        before = dot(jnp.where(chosen, 1.0, 0.0).astype(BF16), upper)
+        place = jnp.where(chosen, before, -1.0)
+        for b in range(2):
+            for k in range(2):
+                row = slice(2 * b + k, 2 * b + k + 1)
+                hit = places == place[row]
+                picks[b, j, k] = jnp.where(hit, 1.0, 0.0).astype(BF16)
+                if k == 0:
+                    value = jnp.sum(jnp.where(hit, weight[row], 0.0), axis=1, keepdims=True)
+                    gate[b, j] = jnp.broadcast_to(value, (capacity, 128))
+
+    def pack_own(q, b):
+        @each_chunk
+        def _(n):
+            at = cols(n, chunk)
+
+            @pl.when(is_inner)
+            def _():
+                snd_p[q, :, at] = dot(picks[b, 0, 1], dense[q, :, at]).astype(BF16)
+                part_copy(q, n).start()
+
+            rows[q, 0, :, at] = dot(picks[b, 0, 0], dense[q, :, at]).astype(BF16)
+
+    def normalise(src, mod, q, keep):
+        @pl.loop(0, count // group)
+        def _(i):
+            at = pl.ds(pl.multiple_of(i * group, group), group)
+            x = src[at, :]
+            centered = x - jnp.mean(x, axis=1, keepdims=True)
+            inv = lax.rsqrt(jnp.mean(centered * centered, axis=1, keepdims=True) + norm_eps)
+            normed = centered * inv
+            dense[q, at, :] = (normed * (1.0 + mod[1]) + mod[0]).astype(BF16)
+            if keep:
+                normed_b[at, :] = normed
+                inv_b[at, :] = jnp.broadcast_to(inv, (group, 128))
+
+    def send_near(q):
+        @pl.when(is_outer)
+        def _():
+            each_chunk(lambda n: near_copy(q, n).start())
+
+    def send_cross(q):
+        @pl.when(is_inner)
+        def _():
+            each_chunk(lambda n: cross_copy(q, 0, n).start())
+
+    def hand_over(q, b):
+        @pl.when(is_inner)
+        def _():
+            @each_chunk
+            def _(n):
+                at = cols(n, chunk)
+                near_copy(q, n).wait_recv()
+                cross_copy(q, 1, n).start()
+                rows[q, 1, :, at] = dot(picks[b, 1, 0], near[q, :, at]).astype(BF16)
+
+    def pass_on(q, b, i, n):
+        at = cols(n, chunk)
+        cross_copy(q, i, n).wait_recv()
+        relay[q, i, :, at] = dot(picks[b, 2 + i, 1], cross[q, i, :, at]).astype(BF16)
+        relay_copy(q, i, n).start()
+        rows[q, 2 + i, :, at] = dot(picks[b, 2 + i, 0], cross[q, i, :, at]).astype(BF16)
+
+    def gather(q, b, i):
+        @pl.when(is_inner)
+        def _():
+            each_chunk(lambda n: pass_on(q, b, i, n))
+
+    def gathered(q):
+        @pl.when(is_outer)
+        def _():
+            @each_chunk
+            def _(n):
+                part_copy(q, n).wait_recv()
+                for i in range(2):
+                    relay_copy(q, i, n).wait_recv()
+
+    def flat(q):
+        return rows[q].reshape(every, width)
+
+    def give(r, n, value):
+        at = cols(n, piece)
+        value = value.astype(BF16).reshape(4, capacity, piece)
+        for j in range(4):
+            res[r, j, :, at] = value[j]
+
+        @pl.when(is_outer)
+        def _():
+            for i in range(2):
+                retx_copy(r, i, n).start()
+
+        @pl.when(is_inner)
+        def _():
+            retp_copy(r, n).start()
+
+    def give_late(r):
+        @pl.when(is_outer)
+        def _():
+            each_piece(lambda n: retp_copy(r, n).start())
+
+    def combine(r, b, n):
+        at = cols(n, piece)
+        for i in range(2):
+            retx_copy(r, i, n).wait_recv()
+            total = dot(picks[b, 2 + i, 0], res[r, 2 + i, :, at], 0, 0) + dot(
+                picks[b, 2 + i, 1], ret_x[r, i, :, at], 0, 0
+            )
+            comb[r, i, :, at] = total.astype(BF16)
+            den_copy(r, i, n).start()
+
+    def own_total(r, b, n):
+        at = cols(n, piece)
+        retp_copy(r, n).wait_recv()
+        den_copy(r, 0, n).wait_recv()
+        return (
+            dot(picks[b, 0, 0], res[r, 0, :, at], 0, 0)
+            + dot(picks[b, 0, 1], ret_p[r, :, at], 0, 0)
+            + den[r, :, at].astype(F32)
+        )
+
+    with scope("bar"):
+        pl.semaphore_wait(barrier, 6)
+    for copy in metas:
+        copy.start()
+    with scope("load0"):
+        loads[0].wait()
+        send_near(OG)
+        send_cross(OG)
+        loads[4].start()
+        loads[3].start()
+    with scope("find0"):
+        find(0)
+    with scope("pk_og"):
+        pack_own(OG, BWD)
+    twin_copy(1, 0, c).start()
+    with scope("norm1"):
+        loads[1].wait()
+        normalise(st_v, bm_ref, HB, True)
+        send_near(HB)
+    twin_copy(1, 1, c).start()
+    with scope("pk_hb"):
+        pack_own(HB, BWD)
+    twin_copy(1, 2, c).start()
+    with scope("norm2"):
+        loads[2].wait()
+
+        @pl.when(s < sections - 1)
+        def _():
+            x_copy.start()
+
+        normalise(x_v, fm_ref, HF, False)
+        send_near(HF)
+        pack_own(HF, FWD)
+    twin_copy(1, 3, c).start()
+    for j in range(1, 4):
+        with scope(f"meta{j}"):
+            remote(
+                meta.at[0], meta.at[j], meta_send.at[j - 1], meta_recv.at[j - 1],
+                s, unit(partner),
+            ).wait_recv()
+            find(j)
+    with scope("over_og"):
+        hand_over(OG, BWD)
+        send_cross(HB)
+    twin_copy(0, 0, c).start()
+    with scope("gat_og0"):
+        gather(OG, BWD, 0)
+    twin_copy(0, 1, c).start()
+    with scope("over_hb"):
+        hand_over(HB, BWD)
+        send_cross(HF)
+    twin_copy(0, 2, c).start()
+    with scope("gat_og1"):
+        gather(OG, BWD, 1)
+    with scope("gathered_og"):
+        gathered(OG)
+    twin_copy(0, 3, c).start()
+
+    with scope("pair"):
+        for j in range(4):
+            @pl.loop(0, width // tile)
+            def _(n):
+                at = cols(n, tile)
+                scaled = bm_ref[2, :, at] * rows[OG, j, :, at].astype(F32)
+                rows[OG, j, :, at] = (gate[BWD, j, :, 0:1] * scaled).astype(BF16)
+
+    with scope("wts"):
+        loads[4].wait()
+        for p in range(shares):
+            twin_copy(1, p, 1 - c).wait_recv()
+
+    with scope("agrad"):
+        for h in range(2):
+            @pl.loop(0, hidden // tile)
+            def _(n):
+                at = pl.ds(pl.multiple_of(h * hidden + n * tile, tile), tile)
+                agrad[:, at] = dot(flat(OG), down[h, cols(n, tile), :], 1, 1)
+
+    with scope("gat_hb0"):
+        gather(HB, BWD, 0)
+    with scope("over_hf"):
+        hand_over(HF, FWD)
+    with scope("gat_hb1"):
+        gather(HB, BWD, 1)
+    with scope("gathered_hb"):
+        gathered(HB)
+        loads[3].wait()
+        for p in range(shares):
+            twin_copy(0, p, 1 - c).wait_recv()
+
+    with scope("pre"):
+        for h in range(2):
+            @pl.loop(0, hidden // tile)
+            def _(n):
+                at = pl.ds(pl.multiple_of(h * hidden + n * tile, tile), tile)
+                pre = dot(flat(HB), up[h, :, cols(n, tile)])
+                t = jnp.tanh(ROOT * (pre + CUBE * pre * pre * pre))
+                slope = ROOT * (1.0 + 3.0 * CUBE * pre * pre)
+                dgelu = 0.5 * (1.0 + t) + 0.5 * pre * (1.0 - t * t) * slope
+                act[:, at] = (agrad[:, at] * dgelu).astype(BF16)
+
+    with scope("partb"):
+        @each_piece
+        def _(n):
+            at = cols(n, piece)
+            give(
+                BWD, n,
+                dot(act[:, :hidden], up[0, at, :], 1, 1)
+                + dot(act[:, hidden:], up[1, at, :], 1, 1),
+            )
+
+        give_late(BWD)
+
+    with scope("gat_hf0"):
+        gather(HF, FWD, 0)
+    with scope("comb_b"):
+        @pl.when(is_inner)
+        def _():
+            per = pieces // chunks
+
+            @each_chunk
+            def _(n):
+                for k in range(per):
+                    combine(BWD, BWD, n * per + k)
+                with scope("gat_hf1"):
+                    pass_on(HF, FWD, 1, n)
+
+    with scope("gathered_hf"):
+        gathered(HF)
+
+    with scope("up"):
+        for h in range(2):
+            @pl.loop(0, hidden // tile)
+            def _(n):
+                at = pl.ds(pl.multiple_of(h * hidden + n * tile, tile), tile)
+                pre = dot(flat(HF), up[h, :, cols(n, tile)])
+                t = jnp.tanh(ROOT * (pre + CUBE * pre * pre * pre))
+                act[:, at] = (0.5 * pre * (1.0 + t)).astype(BF16)
+
+    weight = gate[FWD, :, :, 0:1].reshape(every, 1)
+
+    with scope("down"):
+        @each_piece
+        def _(n):
+            at = cols(n, piece)
+            value = dot(act[:, :hidden], down[0, :, at]) + dot(act[:, hidden:], down[1, :, at])
+            give(FWD, n, weight * value)
+
+        give_late(FWD)
+
+    with scope("comb_f"):
+        @pl.when(is_inner)
+        def _():
+            each_piece(lambda n: combine(FWD, FWD, n))
+
+    @pl.when(s == 0)
+    def _():
+        next_ref[...] = jnp.zeros_like(next_ref)
+
+    @pl.when(s == sections - 1)
+    def _():
+        grad_ref[...] = jnp.zeros_like(grad_ref)
+
+    with scope("own_b"):
+        @each_piece
+        def _(n):
+            dh[:, cols(n, piece)] = own_total(BWD, BWD, n)
+
+    with scope("fin_b"):
+        for p in range(parts):
+            @pl.loop(0, part // group)
+            def _(i):
+                at = pl.ds(pl.multiple_of(p * part + i * group, group), group)
+                dnorm = dh[at, :] * (1.0 + bm_ref[1])
+                normed = normed_b[at, :]
+                one = jnp.mean(dnorm, axis=1, keepdims=True)
+                two = jnp.mean(dnorm * normed, axis=1, keepdims=True)
+                out_b[at, :] = (
+                    dense[OG, at, :].astype(F32) + (dnorm - one - normed * two) * inv_b[at, 0:1]
+                ).astype(BF16)
+
+            @pl.when(s > 0)
+            def _():
+                back_copy(p).start()
+
+    def arrive(n):
+        at = cols(n, piece)
+
+        @pl.when(s > 0)
+        def _():
+            ahead_copy(n).wait_recv()
+            next_ref[:, at] = x_prev[:, at] + m_in[:, at].astype(F32)
+
+    with scope("own_f"):
+        @pl.when(s > 0)
+        def _():
+            x_copy.wait_recv()
+
+        lag = 2
+
+        @each_piece
+        def _(n):
+            at = cols(n, piece)
+            m_out[:, at] = (fm_ref[2, :, at] * own_total(FWD, FWD, n)).astype(BF16)
+
+            @pl.when(s < sections - 1)
+            def _():
+                ahead_copy(n).start()
+
+            @pl.when(n >= lag)
+            def _():
+                arrive(n - lag)
+
+        for n in range(pieces - lag, pieces):
+            arrive(n)
+
+    with scope("tail_send"):
+        for copy in metas:
+            copy.wait_send()
+        for p in range(shares):
+            for w in range(2):
+                twin_copy(w, p, c).wait_send()
+
+        @each_chunk
+        def _(n):
+            for q in range(3):
+                @pl.when(is_outer)
+                def _():
+                    near_copy(q, n).wait_send()
+
+                @pl.when(is_inner)
+                def _():
+                    part_copy(q, n).wait_send()
+                    for i in range(2):
+                        cross_copy(q, i, n).wait_send()
+                        relay_copy(q, i, n).wait_send()
+
+        @each_piece
+        def _(n):
+            for r in range(2):
+                retp_copy(r, n).wait_send()
+
+                @pl.when(is_outer)
+                def _():
+                    for i in range(2):
+                        retx_copy(r, i, n).wait_send()
+
+                @pl.when(is_inner)
+                def _():
+                    for i in range(2):
+                        den_copy(r, i, n).wait_send()
+
+    with scope("tail_hop"):
+        @pl.when(s < sections - 1)
+        def _():
+            x_copy.wait_send()
+            each_piece(lambda n: ahead_copy(n).wait_send())
+            pl.loop(0, parts)(lambda p: back_copy(p).wait_recv())
+
+        @pl.when(s > 0)
+        def _():
+            pl.loop(0, parts)(lambda p: back_copy(p).wait_send())
+
+
+def run_two_sided(
+    section_inputs,
+    stored_inputs,
+    out_grads,
+    fwd_routes,
+    fwd_gates,
+    fwd_modulation,
+    bwd_routes,
+    bwd_gates,
+    bwd_modulation,
+    up_weight,
+    down_weight,
+):
+    sections, units = lax.axis_size("section"), lax.axis_size("expert")
+    experts = units // 2
+    count, width = section_inputs.shape[1:]
+    hidden = up_weight.shape[3]
+    capacity = -(-min(count, 5 * count // (2 * experts)) // 16) * 16
+    every = 4 * capacity
+    chunks, pieces, parts = 4, 8, 4
+
+    def vmem(dtype, *shape):
+        return pltpu.VMEM(shape, dtype)
+
+    def dma(*shape):
+        return pltpu.SemaphoreType.DMA(shape)
+
+    scratch = [
+        vmem(BF16, 2, width, hidden),
+        vmem(BF16, 2, hidden, width),
+        *[vmem(F32, count, width)] * 3,
+        *[vmem(BF16, 3, count, width)] * 2,
+        vmem(BF16, 3, 2, count, width),
+        vmem(BF16, 3, capacity, width),
+        vmem(BF16, 3, 2, capacity, width),
+        vmem(BF16, 3, 4, capacity, width),
+        vmem(BF16, every, 2 * hidden),
+        vmem(F32, every, 2 * hidden),
+        vmem(BF16, 2, 4, capacity, width),
+        vmem(BF16, 2, capacity, width),
+        vmem(BF16, 2, 2, capacity, width),
+        vmem(BF16, 2, 2, count, width),
+        vmem(BF16, 2, count, width),
+        vmem(F32, count, width),
+        vmem(F32, count, 128),
+        *[vmem(BF16, count, width)] * 2,
+        vmem(F32, count, width),
+        vmem(BF16, count, width),
+        vmem(F32, 4, 8, count),
+        vmem(BF16, 2, 4, 2, capacity, count),
+        vmem(F32, 2, 4, capacity, 128),
+        dma(5),
+        *[dma(2, 4)] * 2,
+        *[dma(3)] * 2,
+        *[pltpu.SemaphoreType.DMA] * 2,
+        *[dma(3, chunks)] * 2,
+        *[dma(3, 2, chunks)] * 2,
+        *[dma(3, chunks)] * 2,
+        *[dma(3, 2, chunks)] * 2,
+        *[dma(2, pieces)] * 2,
+        *[dma(2, 2, pieces)] * 2,
+        dma(2, 2, pieces),
+        dma(2, pieces),
+        *[dma(pieces)] * 2,
+        *[dma(parts)] * 2,
+    ]
+    in_vmem = pl.BlockSpec(memory_space=pltpu.VMEM)
+    in_hbm = pl.BlockSpec(memory_space=pl.ANY)
+    flops = 20 * every * width * hidden
+    next_inputs, input_grads = pl.pallas_call(
+        functools.partial(two_sided, sections, units, capacity, chunks, pieces),
+        out_shape=(
+            jax.ShapeDtypeStruct((count, width), F32),
+            jax.ShapeDtypeStruct((count, width), BF16),
+        ),
+        in_specs=[in_hbm] * 3 + [in_vmem] * 6 + [in_hbm] * 2,
+        out_specs=(in_vmem, in_vmem),
+        scratch_shapes=scratch,
+        compiler_params=pltpu.CompilerParams(
+            collective_id=1, has_side_effects=True, vmem_limit_bytes=67043328
+        ),
+        cost_estimate=pl.CostEstimate(
+            flops=flops, bytes_accessed=4 * width * hidden, transcendentals=0
+        ),
+    )(
+        section_inputs[0], stored_inputs[0], out_grads[0],
+        fwd_routes[0].T, fwd_gates[0].T, jnp.transpose(fwd_modulation, (1, 0, 2)),
+        bwd_routes[0].T, bwd_gates[0].T, jnp.transpose(bwd_modulation, (1, 0, 2)),
+        up_weight[0, 0], down_weight[0, 0],
+    )
+    return next_inputs[None], input_grads[None]
+
+
+def on_device(*arrays):
+    sides, inner_and_outer = 2, 2
+    line = lax.axis_size("expert") == 2 * sides * inner_and_outer
+    return (run_two_sided if line else run_many)(*arrays)
+
+
 def solution(mesh):
     tokens = P("section", "expert", None)
     shared = P("section", None, None)

time: 179 us -> 133 us (0.74); the launches traced: 176 us -> 133 us
  Pallas kernels: 164 us -> 128 us
  local copies, waits for them, and re-layouts: 11.2 us -> 4.18 us
    pallas_call x1, Pallas kernels: 164 us -> 128 us  [run_two_sided(): pl.pallas_call(functools.partial(two_sided, sections, units, capacity, ch...]
    unnamed x7 -> x2, local copies, waits for them, and re-layouts: 11.2 us -> 4.18 us
where the time goes in v1:
time: 133 us
  Pallas kernels  128 us (96%)
  local copies, waits for them, and re-layouts  4.18 us (3%)
    pallas_call x1, Pallas kernels, run_two_sided(): pl.pallas_call(functools.partial(two_sided, sections, units, capacity, ch...  128 us
    unnamed x2, local copies, waits for them, and re-layouts  4.18 us

profile of v1, /device:TPU:14, one launch (start us, length us, event | category | flops | bytes accessed | tf_op | source)
XLA Modules:
  0.0 132.8 jit_solution(4183840762495531682)
XLA Ops:
  0.6 127.9 %shard_map.122 = (f32[128,2048]{1,0:T(8,128)}, bf16[128,2048]{1,0:T(8,128)(2,1)}) custom-call(f32[128,2048]{1,0:T(8,128)} %bitcast.25, f32[128,2048]{1,0:T(8,128)} %bitcast.26, bf16[128,2048]{1,0:T(8,128)(2,1)} %bitcast.27, s32[2,128]{1,0:T(2,128)} %bitcast.30, f32[2,128]{1,0:T(2,128)} %bitcast.31, f32[3,1,2048]{2,1,0:T(1,128)} %bitcast.28, ...), custom_call_target="tpu_custom_call" | custom-call | flops 13421772800 | bytes 8388608 | tf_op jit(solution)/shard_map/pallas_call | solution.py:1047
  128.6 2.3 %copy.15 = f32[1,128,2048]{2,1,0:T(8,128)} copy(f32[1,128,2048]{2,1,0:T(8,128)} %bitcast.21) | data formatting | bytes 2097152
  130.9 1.9 %copy.16 = bf16[1,128,2048]{2,1,0:T(8,128)(2,1)} copy(bf16[1,128,2048]{2,1,0:T(8,128)(2,1)} %bitcast.22) | data formatting | bytes 1048576

commit v2 on v1

--- a/solution.py
+++ b/solution.py
@@ -416,15 +416,14 @@
 
 def two_sided(
     sections, units, capacity, chunks, pieces,
-    x_hbm, st_hbm, og_hbm, fr_ref, fg_ref, fm_ref, br_ref, bg_ref, bm_ref, up_hbm, down_hbm,
+    x_hbm, st_hbm, og_hbm, fr_hbm, fg_hbm, fm_hbm, br_hbm, bg_hbm, bm_hbm, up_hbm, down_hbm,
     next_ref, grad_ref,
+    fr_ref, fg_ref, fm_ref, br_ref, bg_ref, bm_ref,
     up, down, x_v, x_prev, st_v, dense, near, cross, snd_p, relay, rows, act, agrad,
     res, ret_p, ret_x, comb, den, normed_b, inv_b, m_out, m_in, dh, out_b,
     meta, picks, gate,
-    load_sem, w_send, w_recv, meta_send, meta_recv, x_send, x_recv, near_send, near_recv,
-    cross_send, cross_recv, part_send, part_recv, relay_send, relay_recv,
-    retp_send, retp_recv, retx_send, retx_recv, den_send, den_recv,
-    sf_send, sf_recv, sb_send, sb_recv,
+    load_sem, small_sem, send_sem, w_recv, meta_send, meta_recv, x_recv, near_recv,
+    cross_recv, rows_recv, retp_recv, retx_recv, den_recv, den_all_recv, sf_recv, sb_recv,
 ):
     s, me = lax.axis_index("section"), lax.axis_index("expert")
     z, c = me // 2, me % 2
@@ -462,7 +461,14 @@
         pltpu.make_async_copy(up_hbm, up.at[c], load_sem.at[3]),
         pltpu.make_async_copy(down_hbm, down.at[c], load_sem.at[4]),
     ]
-    for load in loads[:3]:
+    smalls = [
+        pltpu.make_async_copy(src, dst, small_sem.at[k])
+        for k, (src, dst) in enumerate([
+            (fr_hbm, fr_ref), (fg_hbm, fg_ref), (br_hbm, br_ref), (bg_hbm, bg_ref),
+            (bm_hbm, bm_ref), (fm_hbm, fm_ref),
+        ])
+    ]
+    for load in smalls[:4] + loads[:3] + smalls[4:]:
         load.start()
 
     barrier = pltpu.get_barrier_semaphore()
@@ -475,6 +481,8 @@
             barrier, inc=1, device_id=((s + step) % sections, me), device_id_type=MESH
         )
 
+    for load in smalls[:4]:
+        load.wait()
     meta[0, 0:2, :] = fr_ref[...].astype(F32)
     meta[0, 2:4, :] = fg_ref[...]
     meta[0, 4:6, :] = br_ref[...].astype(F32)
@@ -491,19 +499,26 @@
             s, unit(crossing[1]),
         ),
     ]
-    shares = w_send.shape[1]
-
-    def twin_copy(w, p, slot):
-        src, dst = ((up_hbm, up), (down_hbm, down))[w]
+    shares = 4
+    S_UP, S_DOWN, S_NEAR, S_CROSS, S_PART, S_RELAY, S_RETP, S_RETX, S_DEN, S_AHEAD, S_BACK, S_X = [
+        send_sem.at[k] for k in range(12)
+    ]
+
+    def twin_share(w, p):
+        src, dst, sem = ((up_hbm, up, S_UP), (down_hbm, down, S_DOWN))[w]
         size = src.shape[0] // shares
         at = pl.ds(p * size, size)
-        return remote(src.at[at], dst.at[slot, at], w_send.at[w, p], w_recv.at[w, p], s, twin)
+        return remote(src.at[at], dst.at[c, at], sem, w_recv.at[w], s, twin)
+
+    def twin_whole(w, slot):
+        src, dst, sem = ((up_hbm, up, S_UP), (down_hbm, down, S_DOWN))[w]
+        return remote(src, dst.at[slot], sem, w_recv.at[w], s, twin)
 
     def near_copy(q, n):
         at = cols(n, chunk)
         return remote(
             dense.at[q, :, at], near.at[q, :, at],
-            near_send.at[q, n], near_recv.at[q, n], s, unit(partner),
+            S_NEAR, near_recv.at[q, n], s, unit(partner),
         )
 
     def cross_copy(q, i, n):
@@ -511,60 +526,60 @@
         src = dense if i == 0 else near
         return remote(
             src.at[q, :, at], cross.at[q, i, :, at],
-            cross_send.at[q, i, n], cross_recv.at[q, i, n], s, unit(crossing[0]),
+            S_CROSS, cross_recv.at[q, i, n], s, unit(crossing[0]),
         )
 
     def part_copy(q, n):
         at = cols(n, chunk)
         return remote(
             snd_p.at[q, :, at], rows.at[q, 1, :, at],
-            part_send.at[q, n], part_recv.at[q, n], s, unit(partner),
+            S_PART, rows_recv.at[q], s, unit(partner),
         )
 
     def relay_copy(q, i, n):
         at = cols(n, chunk)
         return remote(
             relay.at[q, i, :, at], rows.at[q, 2 + i, :, at],
-            relay_send.at[q, i, n], relay_recv.at[q, i, n], s, unit(partner),
+            S_RELAY, rows_recv.at[q], s, unit(partner),
         )
 
     def retp_copy(r, n):
         at = cols(n, piece)
         return remote(
             res.at[r, 1, :, at], ret_p.at[r, :, at],
-            retp_send.at[r, n], retp_recv.at[r, n], s, unit(partner),
+            S_RETP, retp_recv.at[r], s, unit(partner),
         )
 
     def retx_copy(r, i, n):
         at = cols(n, piece)
         return remote(
             res.at[r, 2 + i, :, at], ret_x.at[r, i, :, at],
-            retx_send.at[r, i, n], retx_recv.at[r, i, n], s, unit(partner),
+            S_RETX, retx_recv.at[r, n], s, unit(partner),
         )
 
     def den_copy(r, i, n):
         at = cols(n, piece)
         return remote(
             comb.at[r, i, :, at], den.at[r, :, at],
-            den_send.at[r, i, n], den_recv.at[r, n], s, unit(crossing[i]),
-        )
-
-    x_copy = remote(x_v, x_prev, x_send, x_recv, (s + 1) % sections, me)
+            S_DEN, den_all_recv.at[0] if r == BWD else den_recv.at[n], s, unit(crossing[i]),
+        )
+
+    x_copy = remote(x_v, x_prev, S_X, x_recv.at[0], (s + 1) % sections, me)
 
     def ahead_copy(n):
         at = cols(n, piece)
         return remote(
-            m_out.at[:, at], m_in.at[:, at], sf_send.at[n], sf_recv.at[n],
+            m_out.at[:, at], m_in.at[:, at], S_AHEAD, sf_recv.at[n],
             (s + 1) % sections, me,
         )
 
-    parts = sb_send.shape[0]
+    parts = 4
     part = count // parts
 
     def back_copy(p):
         at = cols(p, part)
         return remote(
-            out_b.at[at], grad_ref.at[at], sb_send.at[p], sb_recv.at[p],
+            out_b.at[at], grad_ref.at[at], S_BACK, sb_recv.at[0],
             (s + sections - 1) % sections, me,
         )
 
@@ -662,11 +677,8 @@
     def gathered(q):
         @pl.when(is_outer)
         def _():
-            @each_chunk
-            def _(n):
-                part_copy(q, n).wait_recv()
-                for i in range(2):
-                    relay_copy(q, i, n).wait_recv()
+            got = rows.at[q, 1:4]
+            remote(got, got, S_RELAY, rows_recv.at[q], s, unit(partner)).wait_recv()
 
     def flat(q):
         return rows[q].reshape(every, width)
@@ -682,29 +694,28 @@
             for i in range(2):
                 retx_copy(r, i, n).start()
 
-        @pl.when(is_inner)
-        def _():
-            retp_copy(r, n).start()
-
     def give_late(r):
-        @pl.when(is_outer)
-        def _():
-            each_piece(lambda n: retp_copy(r, n).start())
+        each_piece(lambda n: retp_copy(r, n).start())
 
     def combine(r, b, n):
         at = cols(n, piece)
+        got = ret_x.at[r, :, :, at]
+        remote(got, got, S_RETX, retx_recv.at[r, n], s, unit(partner)).wait_recv()
         for i in range(2):
-            retx_copy(r, i, n).wait_recv()
             total = dot(picks[b, 2 + i, 0], res[r, 2 + i, :, at], 0, 0) + dot(
                 picks[b, 2 + i, 1], ret_x[r, i, :, at], 0, 0
             )
             comb[r, i, :, at] = total.astype(BF16)
             den_copy(r, i, n).start()
 
+    def wait_returned(r):
+        got = ret_p.at[r]
+        remote(got, got, S_RETP, retp_recv.at[r], s, unit(partner)).wait_recv()
+
     def own_total(r, b, n):
         at = cols(n, piece)
-        retp_copy(r, n).wait_recv()
-        den_copy(r, 0, n).wait_recv()
+        if r == FWD:
+            den_copy(r, 0, n).wait_recv()
         return (
             dot(picks[b, 0, 0], res[r, 0, :, at], 0, 0)
             + dot(picks[b, 0, 1], ret_p[r, :, at], 0, 0)
@@ -725,17 +736,19 @@
         find(0)
     with scope("pk_og"):
         pack_own(OG, BWD)
-    twin_copy(1, 0, c).start()
+    twin_share(1, 0).start()
     with scope("norm1"):
         loads[1].wait()
+        smalls[4].wait()
         normalise(st_v, bm_ref, HB, True)
         send_near(HB)
-    twin_copy(1, 1, c).start()
+    twin_share(1, 1).start()
     with scope("pk_hb"):
         pack_own(HB, BWD)
-    twin_copy(1, 2, c).start()
+    twin_share(1, 2).start()
     with scope("norm2"):
         loads[2].wait()
+        smalls[5].wait()
 
         @pl.when(s < sections - 1)
         def _():
@@ -744,7 +757,7 @@
         normalise(x_v, fm_ref, HF, False)
         send_near(HF)
         pack_own(HF, FWD)
-    twin_copy(1, 3, c).start()
+    twin_share(1, 3).start()
     for j in range(1, 4):
         with scope(f"meta{j}"):
             remote(
@@ -755,19 +768,19 @@
     with scope("over_og"):
         hand_over(OG, BWD)
         send_cross(HB)
-    twin_copy(0, 0, c).start()
+    twin_share(0, 0).start()
     with scope("gat_og0"):
         gather(OG, BWD, 0)
-    twin_copy(0, 1, c).start()
+    twin_share(0, 1).start()
     with scope("over_hb"):
         hand_over(HB, BWD)
         send_cross(HF)
-    twin_copy(0, 2, c).start()
+    twin_share(0, 2).start()
     with scope("gat_og1"):
         gather(OG, BWD, 1)
     with scope("gathered_og"):
         gathered(OG)
-    twin_copy(0, 3, c).start()
+    twin_share(0, 3).start()
 
     with scope("pair"):
         for j in range(4):
@@ -779,8 +792,7 @@
 
     with scope("wts"):
         loads[4].wait()
-        for p in range(shares):
-            twin_copy(1, p, 1 - c).wait_recv()
+        twin_whole(1, 1 - c).wait_recv()
 
     with scope("agrad"):
         for h in range(2):
@@ -798,8 +810,7 @@
     with scope("gathered_hb"):
         gathered(HB)
         loads[3].wait()
-        for p in range(shares):
-            twin_copy(0, p, 1 - c).wait_recv()
+        twin_whole(0, 1 - c).wait_recv()
 
     with scope("pre"):
         for h in range(2):
@@ -822,7 +833,9 @@
                 + dot(act[:, hidden:], up[1, at, :], 1, 1),
             )
 
-        give_late(BWD)
+        @pl.when(is_outer)
+        def _():
+            give_late(BWD)
 
     with scope("gat_hf0"):
         gather(HF, FWD, 0)
@@ -837,6 +850,10 @@
                     combine(BWD, BWD, n * per + k)
                 with scope("gat_hf1"):
                     pass_on(HF, FWD, 1, n)
+
+        @pl.when(is_inner)
+        def _():
+            give_late(BWD)
 
     with scope("gathered_hf"):
         gathered(HF)
@@ -875,6 +892,10 @@
         grad_ref[...] = jnp.zeros_like(grad_ref)
 
     with scope("own_b"):
+        wait_returned(BWD)
+        got = den.at[BWD]
+        remote(got, got, S_DEN, den_all_recv.at[0], s, unit(partner)).wait_recv()
+
         @each_piece
         def _(n):
             dh[:, cols(n, piece)] = own_total(BWD, BWD, n)
@@ -909,6 +930,7 @@
         def _():
             x_copy.wait_recv()
 
+        wait_returned(FWD)
         lag = 2
 
         @each_piece
@@ -928,51 +950,37 @@
             arrive(n)
 
     with scope("tail_send"):
+        def sent(sem, src):
+            remote(src, src, sem, rows_recv.at[0], s, unit(partner)).wait_send()
+
         for copy in metas:
             copy.wait_send()
-        for p in range(shares):
-            for w in range(2):
-                twin_copy(w, p, c).wait_send()
-
-        @each_chunk
-        def _(n):
-            for q in range(3):
-                @pl.when(is_outer)
-                def _():
-                    near_copy(q, n).wait_send()
-
-                @pl.when(is_inner)
-                def _():
-                    part_copy(q, n).wait_send()
-                    for i in range(2):
-                        cross_copy(q, i, n).wait_send()
-                        relay_copy(q, i, n).wait_send()
-
-        @each_piece
-        def _(n):
-            for r in range(2):
-                retp_copy(r, n).wait_send()
-
-                @pl.when(is_outer)
-                def _():
-                    for i in range(2):
-                        retx_copy(r, i, n).wait_send()
-
-                @pl.when(is_inner)
-                def _():
-                    for i in range(2):
-                        den_copy(r, i, n).wait_send()
+        for w in range(2):
+            twin_whole(w, c).wait_send()
+        sent(S_RETP, res.at[:, 1])
+
+        @pl.when(is_outer)
+        def _():
+            sent(S_NEAR, dense)
+            sent(S_RETX, res.at[:, 2:4])
+
+        @pl.when(is_inner)
+        def _():
+            sent(S_PART, snd_p)
+            sent(S_CROSS, cross)
+            sent(S_RELAY, relay)
+            sent(S_DEN, comb)
 
     with scope("tail_hop"):
         @pl.when(s < sections - 1)
         def _():
             x_copy.wait_send()
-            each_piece(lambda n: ahead_copy(n).wait_send())
-            pl.loop(0, parts)(lambda p: back_copy(p).wait_recv())
+            sent(S_AHEAD, m_out)
+            remote(grad_ref, grad_ref, S_BACK, sb_recv.at[0], s, twin).wait_recv()
 
         @pl.when(s > 0)
         def _():
-            pl.loop(0, parts)(lambda p: back_copy(p).wait_send())
+            sent(S_BACK, out_b)
 
 
 def run_two_sided(
@@ -994,7 +1002,7 @@
     hidden = up_weight.shape[3]
     capacity = -(-min(count, 5 * count // (2 * experts)) // 16) * 16
     every = 4 * capacity
-    chunks, pieces, parts = 4, 8, 4
+    chunks, pieces = 4, 8
 
     def vmem(dtype, *shape):
         return pltpu.VMEM(shape, dtype)
@@ -1003,6 +1011,12 @@
         return pltpu.SemaphoreType.DMA(shape)
 
     scratch = [
+        vmem(jnp.int32, 2, count),
+        vmem(F32, 2, count),
+        vmem(F32, 3, 1, width),
+        vmem(jnp.int32, 2, count),
+        vmem(F32, 2, count),
+        vmem(F32, 3, 1, width),
         vmem(BF16, 2, width, hidden),
         vmem(BF16, 2, hidden, width),
         *[vmem(F32, count, width)] * 3,
@@ -1027,22 +1041,23 @@
         vmem(BF16, 2, 4, 2, capacity, count),
         vmem(F32, 2, 4, capacity, 128),
         dma(5),
-        *[dma(2, 4)] * 2,
+        dma(6),
+        dma(12),
+        dma(2),
         *[dma(3)] * 2,
-        *[pltpu.SemaphoreType.DMA] * 2,
-        *[dma(3, chunks)] * 2,
-        *[dma(3, 2, chunks)] * 2,
-        *[dma(3, chunks)] * 2,
-        *[dma(3, 2, chunks)] * 2,
-        *[dma(2, pieces)] * 2,
-        *[dma(2, 2, pieces)] * 2,
-        dma(2, 2, pieces),
+        dma(1),
+        dma(3, chunks),
+        dma(3, 2, chunks),
+        dma(3),
+        dma(2),
         dma(2, pieces),
-        *[dma(pieces)] * 2,
-        *[dma(parts)] * 2,
+        dma(pieces),
+        dma(1),
+        dma(pieces),
+        dma(1),
     ]
     in_vmem = pl.BlockSpec(memory_space=pltpu.VMEM)
-    in_hbm = pl.BlockSpec(memory_space=pl.ANY)
+    in_hbm = pl.BlockSpec(memory_space=pltpu.HBM)
     flops = 20 * every * width * hidden
     next_inputs, input_grads = pl.pallas_call(
         functools.partial(two_sided, sections, units, capacity, chunks, pieces),
@@ -1050,21 +1065,21 @@
             jax.ShapeDtypeStruct((count, width), F32),
             jax.ShapeDtypeStruct((count, width), BF16),
         ),
-        in_specs=[in_hbm] * 3 + [in_vmem] * 6 + [in_hbm] * 2,
+        in_specs=[in_hbm] * 11,
         out_specs=(in_vmem, in_vmem),
         scratch_shapes=scratch,
         compiler_params=pltpu.CompilerParams(
-            collective_id=1, has_side_effects=True, vmem_limit_bytes=67043328
+            collective_id=1, has_side_effects=True, vmem_limit_bytes=50 << 20
         ),
         cost_estimate=pl.CostEstimate(
             flops=flops, bytes_accessed=4 * width * hidden, transcendentals=0
         ),
-    )(
+    )(*[pltpu.with_memory_space_constraint(array, pltpu.HBM) for array in (
         section_inputs[0], stored_inputs[0], out_grads[0],
         fwd_routes[0].T, fwd_gates[0].T, jnp.transpose(fwd_modulation, (1, 0, 2)),
         bwd_routes[0].T, bwd_gates[0].T, jnp.transpose(bwd_modulation, (1, 0, 2)),
         up_weight[0, 0], down_weight[0, 0],
-    )
+    )])
     return next_inputs[None], input_grads[None]
 
 

time: 133 us -> 128 us (0.962)
  Pallas kernels: 128 us -> 125 us
  local copies, waits for them, and re-layouts: 4.18 us -> 1.77 us
    pallas_call x1, Pallas kernels: 128 us -> 125 us  [run_two_sided(): pl.pallas_call(functools.partial(two_sided, sections, units, capacity, ch...]
    unnamed x2, local copies, waits for them, and re-layouts: 4.18 us -> 1.77 us
where the time goes in v2:
time: 128 us
  Pallas kernels  125 us (98%)
  local copies, waits for them, and re-layouts  1.77 us (1%)
    pallas_call x1, Pallas kernels, run_two_sided(): pl.pallas_call(functools.partial(two_sided, sections, units, capacity, ch...  125 us

profile of v2, /device:TPU:14, one launch (start us, length us, event | category | flops | bytes accessed | tf_op | source)
XLA Modules:
  0.0 127.5 jit_solution(12318497246679068986)
XLA Ops:
  0.6 125.1 %shard_map.122 = (f32[128,2048]{1,0:T(8,128)S(1)}, bf16[128,2048]{1,0:T(8,128)(2,1)S(1)}) custom-call(f32[128,2048]{1,0:T(8,128)} %bitcast.25, f32[128,2048]{1,0:T(8,128)} %bitcast.26, bf16[128,2048]{1,0:T(8,128)(2,1)} %bitcast.27, s32[2,128]{1,0:T(2,128)} %bitcast.30, f32[2,128]{1,0:T(2,128)} %bitcast.31, f32[3,1,2048]{2,1,0:T(1,128)} %bitcast.28, ...), custom_call_target="tpu_custom_call" | custom-call | flops 13421772800 | bytes 8388608 | tf_op jit(solution)/shard_map/pallas_call | solution.py:1062
  125.7 1.0 copy.15
  126.7 0.8 copy.16

commit v3 on v2

--- a/solution.py
+++ b/solution.py
@@ -422,7 +422,7 @@
     up, down, x_v, x_prev, st_v, dense, near, cross, snd_p, relay, rows, act, agrad,
     res, ret_p, ret_x, comb, den, normed_b, inv_b, m_out, m_in, dh, out_b,
     meta, picks, gate,
-    load_sem, small_sem, send_sem, w_recv, meta_send, meta_recv, x_recv, near_recv,
+    load_sem, small_sem, send_sem, near_send, w_recv, meta_send, meta_recv, x_recv, near_recv,
     cross_recv, rows_recv, retp_recv, retx_recv, den_recv, den_all_recv, sf_recv, sb_recv,
 ):
     s, me = lax.axis_index("section"), lax.axis_index("expert")
@@ -500,9 +500,10 @@
         ),
     ]
     shares = 4
-    S_UP, S_DOWN, S_NEAR, S_CROSS, S_PART, S_RELAY, S_RETP, S_RETX, S_DEN, S_AHEAD, S_BACK, S_X = [
-        send_sem.at[k] for k in range(12)
+    S_UP, S_DOWN, S_CROSS, S_PART, S_RELAY, S_RETP, S_RETX, S_DEN, S_AHEAD, S_BACK, S_X = [
+        send_sem.at[k] for k in range(11)
     ]
+    S_NEAR = near_send
 
     def twin_share(w, p):
         src, dst, sem = ((up_hbm, up, S_UP), (down_hbm, down, S_DOWN))[w]
@@ -518,7 +519,7 @@
         at = cols(n, chunk)
         return remote(
             dense.at[q, :, at], near.at[q, :, at],
-            S_NEAR, near_recv.at[q, n], s, unit(partner),
+            S_NEAR.at[q], near_recv.at[q, n], s, unit(partner),
         )
 
     def cross_copy(q, i, n):
@@ -647,10 +648,10 @@
         def _():
             each_chunk(lambda n: near_copy(q, n).start())
 
-    def send_cross(q):
+    def send_cross(q, first, last):
         @pl.when(is_inner)
         def _():
-            each_chunk(lambda n: cross_copy(q, 0, n).start())
+            pl.loop(first, last)(lambda n: cross_copy(q, 0, n).start())
 
     def hand_over(q, b):
         @pl.when(is_inner)
@@ -729,23 +730,21 @@
     with scope("load0"):
         loads[0].wait()
         send_near(OG)
-        send_cross(OG)
+        send_cross(OG, 0, chunks)
         loads[4].start()
         loads[3].start()
     with scope("find0"):
         find(0)
     with scope("pk_og"):
         pack_own(OG, BWD)
-    twin_share(1, 0).start()
     with scope("norm1"):
         loads[1].wait()
         smalls[4].wait()
         normalise(st_v, bm_ref, HB, True)
         send_near(HB)
-    twin_share(1, 1).start()
+        send_cross(HB, 0, chunks // 2)
     with scope("pk_hb"):
         pack_own(HB, BWD)
-    twin_share(1, 2).start()
     with scope("norm2"):
         loads[2].wait()
         smalls[5].wait()
@@ -757,7 +756,6 @@
         normalise(x_v, fm_ref, HF, False)
         send_near(HF)
         pack_own(HF, FWD)
-    twin_share(1, 3).start()
     for j in range(1, 4):
         with scope(f"meta{j}"):
             remote(
@@ -765,22 +763,47 @@
                 s, unit(partner),
             ).wait_recv()
             find(j)
+    def share(w, p):
+        @pl.when(is_inner)
+        def _():
+            twin_share(w, p).start()
+
+    def near_sent(q):
+        @pl.when(is_outer)
+        def _():
+            remote(
+                dense.at[q], near.at[q], S_NEAR.at[q], near_recv.at[q, 0], s, unit(partner)
+            ).wait_send()
+
+    def share_late(w, first, last):
+        @pl.when(is_outer)
+        def _():
+            for p in range(first, last):
+                twin_share(w, p).start()
+
+    share(1, 0)
     with scope("over_og"):
         hand_over(OG, BWD)
-        send_cross(HB)
-    twin_share(0, 0).start()
+        send_cross(HB, chunks // 2, chunks)
+    share(1, 1)
     with scope("gat_og0"):
         gather(OG, BWD, 0)
-    twin_share(0, 1).start()
+    share(1, 2)
     with scope("over_hb"):
         hand_over(HB, BWD)
-        send_cross(HF)
-    twin_share(0, 2).start()
+        send_cross(HF, 0, chunks)
+    share(1, 3)
     with scope("gat_og1"):
         gather(OG, BWD, 1)
+    share(0, 0)
+    with scope("near_og"):
+        near_sent(OG)
+    share_late(1, 0, 2)
+    with scope("near_hb"):
+        near_sent(HB)
+    share_late(1, 2, 4)
     with scope("gathered_og"):
         gathered(OG)
-    twin_share(0, 3).start()
 
     with scope("pair"):
         for j in range(4):
@@ -790,6 +813,7 @@
                 scaled = bm_ref[2, :, at] * rows[OG, j, :, at].astype(F32)
                 rows[OG, j, :, at] = (gate[BWD, j, :, 0:1] * scaled).astype(BF16)
 
+    share(0, 1)
     with scope("wts"):
         loads[4].wait()
         twin_whole(1, 1 - c).wait_recv()
@@ -801,8 +825,13 @@
                 at = pl.ds(pl.multiple_of(h * hidden + n * tile, tile), tile)
                 agrad[:, at] = dot(flat(OG), down[h, cols(n, tile), :], 1, 1)
 
+    share(0, 2)
+    with scope("near_hf"):
+        near_sent(HF)
+    share_late(0, 0, 4)
     with scope("gat_hb0"):
         gather(HB, BWD, 0)
+    share(0, 3)
     with scope("over_hf"):
         hand_over(HF, FWD)
     with scope("gat_hb1"):
@@ -961,7 +990,6 @@
 
         @pl.when(is_outer)
         def _():
-            sent(S_NEAR, dense)
             sent(S_RETX, res.at[:, 2:4])
 
         @pl.when(is_inner)
@@ -981,6 +1009,17 @@
         @pl.when(s > 0)
         def _():
             sent(S_BACK, out_b)
+
+
+def write_out(next_ref, grad_ref, next_hbm, grad_hbm, sem):
+    copies = [
+        pltpu.make_async_copy(next_ref, next_hbm, sem.at[0]),
+        pltpu.make_async_copy(grad_ref, grad_hbm, sem.at[1]),
+    ]
+    for copy in copies:
+        copy.start()
+    for copy in copies:
+        copy.wait()
 
 
 def run_two_sided(
@@ -1042,7 +1081,8 @@
         vmem(F32, 2, 4, capacity, 128),
         dma(5),
         dma(6),
-        dma(12),
+        dma(11),
+        dma(3),
         dma(2),
         *[dma(3)] * 2,
         dma(1),
@@ -1080,6 +1120,17 @@
         bwd_routes[0].T, bwd_gates[0].T, jnp.transpose(bwd_modulation, (1, 0, 2)),
         up_weight[0, 0], down_weight[0, 0],
     )])
+    next_inputs, input_grads = pl.pallas_call(
+        write_out,
+        out_shape=(
+            jax.ShapeDtypeStruct((count, width), F32),
+            jax.ShapeDtypeStruct((count, width), BF16),
+        ),
+        in_specs=[in_vmem] * 2,
+        out_specs=(in_hbm, in_hbm),
+        scratch_shapes=[dma(2)],
+        compiler_params=pltpu.CompilerParams(vmem_limit_bytes=1 << 20),
+    )(next_inputs, input_grads)
     return next_inputs[None], input_grads[None]
 
 

time: 128 us -> 126 us (0.984)
  local copies, waits for them, and re-layouts: 1.77 us -> 0 us
    unnamed x2 -> x0, local copies, waits for them, and re-layouts: 1.77 us -> none
where the time goes in v3:
time: 126 us
  Pallas kernels  125 us (99%)
    pallas_call x1, Pallas kernels, run_two_sided(): pl.pallas_call(functools.partial(two_sided, sections, units, capacity, ch...  124 us

profile of v3, /device:TPU:14, one launch (start us, length us, event | category | flops | bytes accessed | tf_op | source)
XLA Modules:
  0.0 126.1 jit_solution(914929889427076939)
XLA Ops:
  0.6 124.3 %shard_map.122 = (f32[128,2048]{1,0:T(8,128)S(1)}, bf16[128,2048]{1,0:T(8,128)(2,1)S(1)}) custom-call(f32[128,2048]{1,0:T(8,128)} %bitcast.23, f32[128,2048]{1,0:T(8,128)} %bitcast.24, bf16[128,2048]{1,0:T(8,128)(2,1)} %bitcast.26, s32[2,128]{1,0:T(2,128)} %bitcast.30, f32[2,128]{1,0:T(2,128)} %bitcast.31, f32[3,1,2048]{2,1,0:T(1,128)} %bitcast.28, ...), custom_call_target="tpu_custom_call" | custom-call | flops 13421772800 | bytes 8388608 | tf_op jit(solution)/shard_map/pallas_call | solution.py:1102
  124.9 1.2 shard_map.123

commit v4 on v3

--- a/solution.py
+++ b/solution.py
@@ -868,20 +868,18 @@
 
     with scope("gat_hf0"):
         gather(HF, FWD, 0)
+    with scope("gat_hf1"):
+        @pl.when(is_inner)
+        def _():
+            pl.loop(0, chunks - 1)(lambda n: pass_on(HF, FWD, 1, n))
+
     with scope("comb_b"):
         @pl.when(is_inner)
         def _():
-            per = pieces // chunks
-
-            @each_chunk
-            def _(n):
-                for k in range(per):
-                    combine(BWD, BWD, n * per + k)
-                with scope("gat_hf1"):
-                    pass_on(HF, FWD, 1, n)
-
-        @pl.when(is_inner)
-        def _():
+            early = pieces // chunks
+            pl.loop(0, early)(lambda n: combine(BWD, BWD, n))
+            pass_on(HF, FWD, 1, chunks - 1)
+            pl.loop(early, pieces)(lambda n: combine(BWD, BWD, n))
             give_late(BWD)
 
     with scope("gathered_hf"):
@@ -910,7 +908,7 @@
     with scope("comb_f"):
         @pl.when(is_inner)
         def _():
-            each_piece(lambda n: combine(FWD, FWD, n))
+            pl.loop(0, pieces // 2)(lambda n: combine(FWD, FWD, n))
 
     @pl.when(s == 0)
     def _():
@@ -945,6 +943,11 @@
             @pl.when(s > 0)
             def _():
                 back_copy(p).start()
+
+    with scope("comb_f2"):
+        @pl.when(is_inner)
+        def _():
+            pl.loop(pieces // 2, pieces)(lambda n: combine(FWD, FWD, n))
 
     def arrive(n):
         at = cols(n, piece)

time: 126 us -> 125 us (level)
  the two profiles are of different devices: /device:TPU:14 before, /device:TPU:0 now
where the time goes in v4:
time: 125 us
  Pallas kernels  124 us (99%)
    pallas_call x1, Pallas kernels, run_two_sided(): pl.pallas_call(functools.partial(two_sided, sections, units, capacity, ch...  123 us

profile of v4, /device:TPU:0, one launch (start us, length us, event | category | flops | bytes accessed | tf_op | source)
XLA Modules:
  0.0 124.6 jit_solution(133599111180467449)
XLA Ops:
  0.6 122.8 %shard_map.122 = (f32[128,2048]{1,0:T(8,128)S(1)}, bf16[128,2048]{1,0:T(8,128)(2,1)S(1)}) custom-call(f32[128,2048]{1,0:T(8,128)} %bitcast.23, f32[128,2048]{1,0:T(8,128)} %bitcast.24, bf16[128,2048]{1,0:T(8,128)(2,1)} %bitcast.26, s32[2,128]{1,0:T(2,128)} %bitcast.30, f32[2,128]{1,0:T(2,128)} %bitcast.31, f32[3,1,2048]{2,1,0:T(1,128)} %bitcast.28, ...), custom_call_target="tpu_custom_call" | custom-call | flops 13421772800 | bytes 8388608 | tf_op jit(solution)/shard_map/pallas_call | solution.py:1105
  123.5 1.2 shard_map.123

commit v5 on v4

--- a/solution.py
+++ b/solution.py
@@ -454,6 +454,16 @@
     def cols(n, size):
         return pl.ds(pl.multiple_of(n * size, size), size)
 
+    barrier = pltpu.get_barrier_semaphore()
+    for chip in (partner, crossing[0], crossing[1]):
+        pl.semaphore_signal(barrier, inc=1, device_id=(s, unit(chip)), device_id_type=MESH)
+    twin = me + 1 - 2 * c
+    pl.semaphore_signal(barrier, inc=1, device_id=(s, twin), device_id_type=MESH)
+    for step in (1, sections - 1):
+        pl.semaphore_signal(
+            barrier, inc=1, device_id=((s + step) % sections, me), device_id_type=MESH
+        )
+
     loads = [
         pltpu.make_async_copy(og_hbm, dense.at[OG], load_sem.at[0]),
         pltpu.make_async_copy(st_hbm, st_v, load_sem.at[1]),
@@ -471,16 +481,6 @@
     for load in smalls[:4] + loads[:3] + smalls[4:]:
         load.start()
 
-    barrier = pltpu.get_barrier_semaphore()
-    for chip in (partner, crossing[0], crossing[1]):
-        pl.semaphore_signal(barrier, inc=1, device_id=(s, unit(chip)), device_id_type=MESH)
-    twin = me + 1 - 2 * c
-    pl.semaphore_signal(barrier, inc=1, device_id=(s, twin), device_id_type=MESH)
-    for step in (1, sections - 1):
-        pl.semaphore_signal(
-            barrier, inc=1, device_id=((s + step) % sections, me), device_id_type=MESH
-        )
-
     for load in smalls[:4]:
         load.wait()
     meta[0, 0:2, :] = fr_ref[...].astype(F32)
@@ -702,7 +702,7 @@
         at = cols(n, piece)
         got = ret_x.at[r, :, :, at]
         remote(got, got, S_RETX, retx_recv.at[r, n], s, unit(partner)).wait_recv()
-        for i in range(2):
+        for i in (1, 0):
             total = dot(picks[b, 2 + i, 0], res[r, 2 + i, :, at], 0, 0) + dot(
                 picks[b, 2 + i, 1], ret_x[r, i, :, at], 0, 0
             )

time: 125 us -> 124 us (level)
  the two profiles are of different devices: /device:TPU:0 before, /device:TPU:14 now
where the time goes in v5:
time: 124 us; the launch traced here: 122 us
  Pallas kernels  122 us (98%)
    pallas_call x1, Pallas kernels, run_two_sided(): pl.pallas_call(functools.partial(two_sided, sections, units, capacity, ch...  120 us

profile of v5, /device:TPU:14, one launch (start us, length us, event | category | flops | bytes accessed | tf_op | source)
XLA Modules:
  0.0 122.2 jit_solution(7702068016289842831)
XLA Ops:
  0.6 120.4 %shard_map.122 = (f32[128,2048]{1,0:T(8,128)S(1)}, bf16[128,2048]{1,0:T(8,128)(2,1)S(1)}) custom-call(f32[128,2048]{1,0:T(8,128)} %bitcast.23, f32[128,2048]{1,0:T(8,128)} %bitcast.24, bf16[128,2048]{1,0:T(8,128)(2,1)} %bitcast.26, s32[2,128]{1,0:T(2,128)} %bitcast.30, f32[2,128]{1,0:T(2,128)} %bitcast.31, f32[3,1,2048]{2,1,0:T(1,128)} %bitcast.28, ...), custom_call_target="tpu_custom_call" | custom-call | flops 13421772800 | bytes 8388608 | tf_op jit(solution)/shard_map/pallas_call | solution.py:1105
  121.0 1.2 shard_map.123
